TPU v7x, 32 devices: a whole 2x2x4 slice. The times are simulated.
32 devices in a mesh: shard: 8 (over z, x), model: 4 (over y, core).
Axes of the slice: x: 2, y: 2, z: 4, core: 2. Of those that a mesh axis runs over, the one named last changes fastest.
Arguments:
- grad_stack: float32 [64, 128, 2048], P(None, 'shard', 'model'), may hold values from -6 to 6
- moment_stack: float32 [64, 128, 2048], P(None, 'shard', 'model'), may hold values from -6 to 6
- weight_stack: float32 [64, 128, 2048], P(None, 'shard', 'model'), may hold values from -0.1875 to 0.1875
Outputs:
- new_weights: float32 [64, 128, 2048], P(None, 'shard', 'model')
- new_momentum: float32 [64, 128, 2048], P(None, 'shard', 'model')
All inputs are finite; a program needn't handle non-finite values.
Results may differ from a plain program's by a relative error of at most 0.00021.
Values sent between devices are 32-bit elements; how exact they have to be, the bound alone decides.
A program may use at most 64 MiB of HBM per device.

v0:
```python
import jax
import jax.numpy as jnp
from jax import lax
from jax.sharding import PartitionSpec as P

ITERS = 5


hold_rate = 0.95
learn_rate = 1.0
decay_rate = 0.1


def on_device(grad_stack, moment_stack, weight_stack):
    new_momentum = hold_rate * moment_stack + grad_stack
    moved = lax.all_to_all(new_momentum, "shard", split_axis=0, concat_axis=1, tiled=True)
    whole = lax.all_to_all(moved, "model", split_axis=0, concat_axis=2, tiled=True)
    iterate = whole * lax.rsqrt(jnp.sum(whole * whole, axis=(1, 2), keepdims=True) + 1e-06)
    for step in range(ITERS):
        gram = jnp.einsum("mik,mjk->mij", iterate, iterate, precision=lax.Precision.HIGHEST)
        mixed = -4.775 * gram + 2.0315 * jnp.einsum(
            "mij,mjk->mik", gram, gram, precision=lax.Precision.HIGHEST
        )
        iterate = 3.4445 * iterate + jnp.einsum(
            "mij,mjk->mik", mixed, iterate, precision=lax.Precision.HIGHEST
        )
    iterate = lax.all_to_all(iterate, "model", split_axis=2, concat_axis=0, tiled=True)
    back = lax.all_to_all(iterate, "shard", split_axis=1, concat_axis=0, tiled=True)
    new_weights = (1.0 - learn_rate * decay_rate) * weight_stack - learn_rate * back
    return (new_weights, new_momentum)


def solution(mesh):
    in_specs = (P(None, "shard", "model"), P(None, "shard", "model"), P(None, "shard", "model"))
    out_specs = (P(None, "shard", "model"), P(None, "shard", "model"))
    return jax.shard_map(
        on_device, mesh=mesh, in_specs=in_specs, out_specs=out_specs, check_vma=False
    )
```

profile of v0, /device:TPU:0, one launch (start us, length us, event | category | flops | bytes accessed | tf_op | source)
XLA Modules:
  0.0 201.4 jit_solution(9015392029939846904)
XLA Ops:
  0.6 2.7 %multiply_add_fusion = f32[64,16,512]{2,1,0:T(8,128)S(1)} fusion(f32[64,16,512]{2,1,0:T(8,128)} %param.3, f32[64,16,512]{2,1,0:T(8,128)} %param.4), kind=kLoop, calls=%fused_computation.7 | loop fusion | flops 1048576 | bytes 6291456 | tf_op jit(solution)/shard_map/add | solution.py:15
  3.4 55.3 %all_to_all.72 = f32[64,16,512]{2,1,0:T(8,128)S(1)} all-to-all(f32[64,16,512]{2,1,0:T(8,128)S(1)} %multiply_add_fusion), channel_id=1, replica_groups=mesh['shard'=8,'model'=4] {'shard'}, dimensions={0} | all-to-all | bytes 4194304 | tf_op jit(solution)/shard_map/all_to_all | solution.py:16
  58.9 28.3 %all_to_all.73 = f32[8,128,512]{2,1,0:T(8,128)S(1)} all-to-all(f32[8,128,512]{2,1,0:T(8,128)S(1)} %bitcast.49), channel_id=1, replica_groups=mesh['shard'=8,'model'=4] {'model'}, dimensions={0} | all-to-all | bytes 4194304 | tf_op jit(solution)/shard_map/all_to_all | solution.py:17
  87.1 0.4 multiply_reduce_fusion
  87.7 2.3 %fusion = f32[2,128,128]{2,1,0:T(8,128)S(1)} fusion(f32[2,128,2048]{2,1,0:T(8,128)S(1)} %bitcast.45, f32[2]{0:T(128)S(1)} %add_rsqrt_fusion), kind=kOutput, calls=%fused_computation.8 | convolution fusion | flops 805830656 | bytes 2228232 | tf_op jit(solution)/shard_map/mik,mjk->mij/dot_general | solution.py:20
  90.0 0.3 fusion.7
  90.3 2.1 %convolution_add_fusion.4 = f32[2,128,2048]{2,1,0:T(8,128)S(1)} fusion(f32[2,128,128]{2,1,0:T(8,128)S(1)} %fusion.7, f32[2,128,2048]{2,1,0:T(8,128)S(1)} %bitcast.46, f32[2]{0:T(128)S(1)} %add_rsqrt_fusion), kind=kOutput, calls=%fused_computation.4 | convolution fusion | flops 807403520 | bytes 4325384 | tf_op jit(solution)/shard_map/mij,mjk->mik/dot_general | solution.py:24
  92.4 2.0 %fusion.10 = f32[2,128,128]{2,1,0:T(8,128)S(1)} fusion(f32[2,128,2048]{2,1,0:T(8,128)S(1)} %convolution_add_fusion.4), kind=kOutput, calls=%fused_computation.24 | convolution fusion | flops 805306368 | bytes 2228224 | tf_op jit(solution)/shard_map/mik,mjk->mij/dot_general | solution.py:20
  94.5 0.3 fusion.6
  94.7 2.1 %convolution_add_fusion.3 = f32[2,128,2048]{2,1,0:T(8,128)S(1)} fusion(f32[2,128,128]{2,1,0:T(8,128)S(1)} %fusion.6, f32[2,128,2048]{2,1,0:T(8,128)S(1)} %convolution_add_fusion.4), kind=kOutput, calls=%fused_computation.3 | convolution fusion | flops 806354944 | bytes 4325376 | tf_op jit(solution)/shard_map/mij,mjk->mik/dot_general | solution.py:24
  96.8 2.0 %fusion.11 = f32[2,128,128]{2,1,0:T(8,128)S(1)} fusion(f32[2,128,2048]{2,1,0:T(8,128)S(1)} %convolution_add_fusion.3), kind=kOutput, calls=%fused_computation.25 | convolution fusion | flops 805306368 | bytes 2228224 | tf_op jit(solution)/shard_map/mik,mjk->mij/dot_general | solution.py:20
  99.2 2.3 %convolution_add_fusion.2 = f32[2,128,2048]{2,1,0:T(8,128)S(1)} fusion(f32[2,128,128]{2,1,0:T(8,128)S(1)} %fusion.5, f32[2,128,2048]{2,1,0:T(8,128)S(1)} %convolution_add_fusion.3), kind=kOutput, calls=%fused_computation.2 | convolution fusion | flops 806354944 | bytes 4325376 | tf_op jit(solution)/shard_map/mij,mjk->mik/dot_general | solution.py:24
  101.5 2.0 %fusion.12 = f32[2,128,128]{2,1,0:T(8,128)S(1)} fusion(f32[2,128,2048]{2,1,0:T(8,128)S(1)} %convolution_add_fusion.2), kind=kOutput, calls=%fused_computation.26 | convolution fusion | flops 805306368 | bytes 2228224 | tf_op jit(solution)/shard_map/mik,mjk->mij/dot_general | solution.py:20
  103.8 2.1 %convolution_add_fusion.1 = f32[2,128,2048]{2,1,0:T(8,128)S(1)} fusion(f32[2,128,128]{2,1,0:T(8,128)S(1)} %fusion.4, f32[2,128,2048]{2,1,0:T(8,128)S(1)} %convolution_add_fusion.2), kind=kOutput, calls=%fused_computation.1 | convolution fusion | flops 806354944 | bytes 4325376 | tf_op jit(solution)/shard_map/mij,mjk->mik/dot_general | solution.py:24
  105.9 2.0 %fusion.13 = f32[2,128,128]{2,1,0:T(8,128)S(1)} fusion(f32[2,128,2048]{2,1,0:T(8,128)S(1)} %convolution_add_fusion.1), kind=kOutput, calls=%fused_computation.27 | convolution fusion | flops 805306368 | bytes 2228224 | tf_op jit(solution)/shard_map/mik,mjk->mij/dot_general | solution.py:20
  108.2 2.1 %convolution_add_fusion = f32[2,128,2048]{2,1,0:T(8,128)S(1)} fusion(f32[2,128,128]{2,1,0:T(8,128)S(1)} %fusion.3, f32[2,128,2048]{2,1,0:T(8,128)S(1)} %convolution_add_fusion.1), kind=kOutput, calls=%fused_computation | convolution fusion | flops 806354944 | bytes 4325376 | tf_op jit(solution)/shard_map/mij,mjk->mik/dot_general | solution.py:24
  110.3 2.3 %copy.19 = f32[2,128,2048]{1,0,2:T(2,128)} copy(f32[2,128,2048]{2,1,0:T(8,128)S(1)} %convolution_add_fusion) | data formatting | bytes 4194304 | tf_op jit(solution)/shard_map/add | solution.py:24
  112.6 29.2 %all_to_all.74 = f32[2,128,2048]{1,0,2:T(2,128)S(1)} all-to-all(f32[2,128,2048]{1,0,2:T(2,128)} %copy.19), channel_id=1, replica_groups=mesh['shard'=8,'model'=4] {'model'}, dimensions={2} | all-to-all | bytes 4194304 | tf_op jit(solution)/shard_map/all_to_all | solution.py:27
  142.0 1.8 copy.21
  143.8 2.8 %copy.22 = f32[8,128,512]{2,0,1:T(8,128)S(1)} copy(f32[8,128,512]{2,1,0:T(8,128)} %bitcast.51) | data formatting | bytes 4194304 | tf_op jit(solution)/shard_map/all_to_all | solution.py:27
  146.6 51.4 %all_to_all.75 = f32[8,128,512]{2,0,1:T(8,128)S(1)} all-to-all(f32[8,128,512]{2,0,1:T(8,128)S(1)} %copy.22), channel_id=1, replica_groups=mesh['shard'=8,'model'=4] {'shard'}, dimensions={1} | all-to-all | bytes 4194304 | tf_op jit(solution)/shard_map/all_to_all | solution.py:28
  198.0 1.2 copy.24
  199.2 0.4 copy-done.1
  199.5 1.8 bitcast_subtract_fusion
  (10 shorter events, 1.4 us)
Async XLA Ops:
  3.3 55.3 %copy-start = (f32[64,16,512]{2,1,0:T(8,128)}, f32[64,16,512]{2,1,0:T(8,128)S(1)}, u32[]{:S(2)}) copy-start(f32[64,16,512]{2,1,0:T(8,128)S(1)} %multiply_add_fusion) | copy-start | bytes 6291460
  198.0 1.6 copy-start.1
where the time goes:
time: 202 us; the launch traced here: 201 us
  blocking collectives  164 us (81%)
  matrix products  22.4 us (11%)
  local copies, waits for them, and re-layouts  9.08 us (4%)
  other arithmetic  4.91 us (2%)
    all_to_all x1, blocking collectives, on_device(): lax.all_to_all(new_momentum, 'shard', split_axis=0, concat_axis=1, tiled=...  55.3 us
    all_to_all x1, blocking collectives, on_device(): lax.all_to_all(iterate, 'shard', split_axis=1, concat_axis=0, tiled=True)  51.4 us
    all_to_all x1, blocking collectives, on_device(): lax.all_to_all(iterate, 'model', split_axis=2, concat_axis=0, tiled=True)  29.2 us
    all_to_all x1, blocking collectives, on_device(): lax.all_to_all(moved, 'model', split_axis=0, concat_axis=2, tiled=True)  28.3 us
    dot_general x5, matrix products, on_device(): jnp.einsum('mij,mjk->mik', mixed, iterate, precision=lax.Precision.HIGHEST)  10.7 us
    dot_general x5, matrix products, on_device(): jnp.einsum('mik,mjk->mij', iterate, iterate, precision=lax.Precision.HIGH...  10.4 us
    all_to_all x3, local copies, waits for them, and re-layouts, on_device(): lax.all_to_all(iterate, 'model', split_axis=2, concat_axis=0, tiled=True)  4.76 us

commit v1 on v0

v1 whole, which is shorter than its diff:
```python
import jax
import jax.numpy as jnp
from jax import lax
from jax.sharding import PartitionSpec as P

ITERS = 5


hold_rate = 0.95
learn_rate = 1.0
decay_rate = 0.1
HIGH = lax.Precision.HIGHEST


def batched(a, b):
    return jnp.einsum("mij,mjk->mik", a, b, precision=HIGH)


def polynomial(gram):
    size = jnp.trace(gram, axis1=1, axis2=2)[:, None, None]
    scale = lax.rsqrt(size + 1e-06)
    gram = gram * (scale * scale)
    eye = jnp.eye(gram.shape[-1], dtype=gram.dtype)
    total = None
    for step in range(ITERS):
        factor = 3.4445 * eye + (-4.775 * gram + 2.0315 * batched(gram, gram))
        total = factor if total is None else batched(factor, total)
        if step < ITERS - 1:
            gram = batched(factor, batched(gram, factor))
    return total * scale


def on_device(grad_stack, moment_stack, weight_stack):
    new_momentum = hold_rate * moment_stack + grad_stack
    moved = lax.all_to_all(new_momentum, "shard", split_axis=0, concat_axis=1, tiled=True)
    part = jnp.einsum("mik,mjk->mij", moved, moved, precision=HIGH)
    parts = lax.axis_size("model")
    part = part.reshape((parts, part.shape[0] // parts) + part.shape[1:])
    gram = jnp.sum(lax.all_to_all(part, "model", split_axis=0, concat_axis=0), axis=0)
    mixed = lax.all_gather(polynomial(gram), "model", axis=0, tiled=True)
    iterate = batched(mixed, moved)
    back = lax.all_to_all(iterate, "shard", split_axis=1, concat_axis=0, tiled=True)
    new_weights = (1.0 - learn_rate * decay_rate) * weight_stack - learn_rate * back
    return (new_weights, new_momentum)


def solution(mesh):
    in_specs = (P(None, "shard", "model"), P(None, "shard", "model"), P(None, "shard", "model"))
    out_specs = (P(None, "shard", "model"), P(None, "shard", "model"))
    return jax.shard_map(
        on_device, mesh=mesh, in_specs=in_specs, out_specs=out_specs, check_vma=False
    )
```

time: 202 us -> 144 us (0.71)
  blocking collectives: 164 us -> 114 us
  matrix products: 22.4 us -> 9.4 us
  waiting for transfers between devices: 0 us -> 8.74 us
  local copies, waits for them, and re-layouts: 9.08 us -> 2.99 us
  starting transfers between devices: 0 us -> 3.47 us
    all_to_all x2 -> x0, blocking collectives: 57.5 us -> none  [the longest x1 29.2 us: on_device(): lax.all_to_all(iterate, 'model', split_axis=2, concat_axis=0, tiled=True)]
    dot_general x15 -> x19, matrix products: 22.4 us -> 9.4 us  [the longest x18 6.54 us: batched(): return jnp.einsum('mij,mjk->mik', a, b, precision=HIGH)]
    all_to_all x0 -> x1, waiting for transfers between devices: none -> 8.74 us  [on_device(): lax.all_to_all(part, 'model', split_axis=0, concat_axis=0)]
    all_gather x0 -> x1, blocking collectives: none -> 6.5 us  [on_device(): mixed = lax.all_gather(polynomial(gram), 'model', axis=0, tiled=True)]
    all_to_all x4 -> x0, local copies, waits for them, and re-layouts: 5 us -> none  [the longest x3 4.76 us: on_device(): lax.all_to_all(iterate, 'model', split_axis=2, concat_axis=0, tiled=True)]
    all_to_all x0 -> x1, starting transfers between devices: none -> 3.47 us  [on_device(): lax.all_to_all(part, 'model', split_axis=0, concat_axis=0)]
    add x1 -> x0, local copies, waits for them, and re-layouts: 2.32 us -> none  [on_device(): 3.4445 * iterate]
  transfers between devices with their start and end apart: 0 -> 1, of which waited for: 0 -> 1; matrix products, arithmetic and copies ran while one was open for 0% -> 0% of each run, Pallas kernels for 0% -> 0%
where the time goes in v1:
time: 144 us
  blocking collectives  114 us (79%)
  matrix products  9.4 us (7%)
  waiting for transfers between devices  8.74 us (6%)
  other arithmetic  4.71 us (3%)
  starting transfers between devices  3.47 us (2%)
  local copies, waits for them, and re-layouts  2.99 us (2%)
    all_to_all x1, blocking collectives, on_device(): lax.all_to_all(new_momentum, 'shard', split_axis=0, concat_axis=1, tiled=...  55.3 us
    all_to_all x1, blocking collectives, on_device(): lax.all_to_all(iterate, 'shard', split_axis=1, concat_axis=0, tiled=True)  52.1 us
    all_to_all x1, waiting for transfers between devices, on_device(): lax.all_to_all(part, 'model', split_axis=0, concat_axis=0)  8.74 us
    dot_general x18, matrix products, batched(): return jnp.einsum('mij,mjk->mik', a, b, precision=HIGH)  6.54 us
    all_gather x1, blocking collectives, on_device(): mixed = lax.all_gather(polynomial(gram), 'model', axis=0, tiled=True)  6.5 us
    all_to_all x1, starting transfers between devices, on_device(): lax.all_to_all(part, 'model', split_axis=0, concat_axis=0)  3.47 us
  transfers between devices with their start and end apart: 1, of which 1 were waited for; matrix products, arithmetic and copies ran while one was open for 0% of the time, Pallas kernels for 0%

profile of v1, /device:TPU:0, one launch (start us, length us, event | category | flops | bytes accessed | tf_op | source)
XLA Modules:
  0.0 144.1 jit_solution(6132666401640892697)
XLA Ops:
  0.6 2.7 %multiply_add_fusion = f32[64,16,512]{2,1,0:T(8,128)S(1)} fusion(f32[64,16,512]{2,1,0:T(8,128)} %param.3, f32[64,16,512]{2,1,0:T(8,128)} %param.4), kind=kLoop, calls=%fused_computation.1 | loop fusion | flops 1048576 | bytes 6291456 | tf_op jit(solution)/shard_map/add | solution.py:34
  3.4 55.3 %all_to_all.41 = f32[64,16,512]{2,1,0:T(8,128)S(1)} all-to-all(f32[64,16,512]{2,1,0:T(8,128)S(1)} %multiply_add_fusion), channel_id=1, replica_groups=mesh['shard'=8,'model'=4] {'shard'}, dimensions={0} | all-to-all | bytes 4194304 | tf_op jit(solution)/shard_map/all_to_all | solution.py:35
  58.9 2.9 %fusion.16 = f32[8,128,128]{2,1,0:T(8,128)} fusion(f32[8,128,512]{2,1,0:T(8,128)S(1)} %bitcast.45), kind=kOutput, calls=%fused_computation.28 | convolution fusion | flops 805306368 | bytes 2621440 | tf_op jit(solution)/shard_map/mik,mjk->mij/dot_general | solution.py:36
  61.7 3.5 %all-to-all-start.1 = ((f32[4,2,128,128]{3,2,1,0:T(8,128)}), f32[4,2,128,128]{3,2,1,0:T(8,128)S(1)}, u32[]{:S(2)}, u32[]{:S(2)}) async-start(f32[4,2,128,128]{3,2,1,0:T(8,128)} %bitcast.3), calls=%async_computation.1 | async-start | bytes 1048576 | tf_op jit(solution)/shard_map/all_to_all | solution.py:39
  65.2 8.7 %all-to-all-done.1 = f32[4,2,128,128]{3,2,1,0:T(8,128)S(1)} async-done(((f32[4,2,128,128]{3,2,1,0:T(8,128)}), f32[4,2,128,128]{3,2,1,0:T(8,128)S(1)}, u32[]{:S(2)}, u32[]{:S(2)}) %all-to-all-start.1) | async-done | bytes 524320 | tf_op jit(solution)/shard_map/all_to_all | solution.py:39
  74.1 0.4 fusion.9
  74.5 0.3 fusion.11
  74.8 0.3 fusion.17
  75.1 0.3 fusion.7
  75.4 0.3 fusion.24
  75.9 0.3 fusion.19
  76.2 0.3 fusion.5
  77.0 0.3 fusion.21
  77.3 0.3 fusion.3
  77.6 0.3 fusion.22
  78.4 0.3 fusion.1
  78.7 0.3 convolution_multiply_fusion
  79.0 6.5 %all_gather.3 = f32[8,128,128]{2,1,0:T(8,128)S(1)} all-gather(f32[2,128,128]{2,1,0:T(8,128)S(1)} %convolution_multiply_fusion), channel_id=1, replica_groups=mesh['shard'=8,'model'=4] {'model'}, dimensions={0}, use_global_device_ids=true | all-gather | bytes 655360 | tf_op jit(solution)/shard_map/all_gather | solution.py:40
  85.5 1.9 %fusion.27 = f32[8,128,512]{2,1,0:T(8,128)S(1)} fusion(f32[8,128,128]{2,1,0:T(8,128)S(1)} %all_gather.3, f32[8,128,512]{2,1,0:T(8,128)S(1)} %bitcast.46), kind=kOutput, calls=%fused_computation.39 | convolution fusion | flops 805306368 | bytes 4718592 | tf_op jit(solution)/shard_map/mij,mjk->mik/dot_general | solution.py:16
  87.3 1.2 copy.8
  88.6 52.1 %all_to_all.42 = f32[8,128,512]{2,0,1:T(8,128)S(1)} all-to-all(f32[8,128,512]{2,0,1:T(8,128)S(1)} %copy.8), channel_id=1, replica_groups=mesh['shard'=8,'model'=4] {'shard'}, dimensions={1} | all-to-all | bytes 4194304 | tf_op jit(solution)/shard_map/all_to_all | solution.py:42
  140.7 1.2 copy.9
  141.9 0.4 copy-done.1
  142.2 1.8 %bitcast_subtract_fusion = f32[64,16,512]{2,1,0:T(8,128)} fusion(f32[8,8,16,512]{3,2,1,0:T(8,128)S(1)} %copy.9, f32[64,16,512]{2,1,0:T(8,128)S(1)} %copy-done.1), kind=kLoop, calls=%fused_computation | loop fusion | flops 1048576 | bytes 6291456 | tf_op jit(solution)/shard_map/sub | solution.py:43
  (14 shorter events, 1.7 us)
Async XLA Ops:
  3.3 55.3 %copy-start = (f32[64,16,512]{2,1,0:T(8,128)}, f32[64,16,512]{2,1,0:T(8,128)S(1)}, u32[]{:S(2)}) copy-start(f32[64,16,512]{2,1,0:T(8,128)S(1)} %multiply_add_fusion) | copy-start | bytes 6291460
  61.7 12.3 %all-to-all-start.1 = ((f32[4,2,128,128]{3,2,1,0:T(8,128)}), f32[4,2,128,128]{3,2,1,0:T(8,128)S(1)}, u32[]{:S(2)}, u32[]{:S(2)}) async-start(f32[4,2,128,128]{3,2,1,0:T(8,128)} %bitcast.3), calls=%async_computation.1 | async-start | bytes 1048576 | tf_op jit(solution)/shard_map/all_to_all | solution.py:39
  140.7 1.6 %copy-start.1 = (f32[64,16,512]{2,1,0:T(8,128)S(1)}, f32[64,16,512]{2,1,0:T(8,128)}, u32[]{:S(2)}) copy-start(f32[64,16,512]{2,1,0:T(8,128)} %param.5) | copy-start | bytes 6291460
